TPU v7x, 32 devices: a whole 2x2x4 slice. The times are simulated.
32 devices in a mesh: dp: 8 (over y, x, core), mp: 4 (over z).
Axes of the slice: x: 2, y: 2, z: 4, core: 2. Of those that a mesh axis runs over, the one named last changes fastest.
Arguments:
- tokens: bfloat16 [16384, 1024], P(('dp', 'mp')), may hold values from -6 to 6
- norm_gain: float32 [2, 1024], replicated, may hold values from 0.1 to 1.9
- qkv_weight: bfloat16 [3, 1024, 1024], P(None, 'dp', 'mp')
- out_weight: bfloat16 [1024, 1024], P('mp', 'dp'), may hold values from -0.1875 to 0.1875
- variate_bias: float32 [2, 16], replicated, may hold values from -6 to 6
- ffn_weight: bfloat16 [2, 1024, 2816], P(None, 'dp', 'mp'), may hold values from -0.1875 to 0.1875
- down_weight: bfloat16 [2816, 1024], P('mp', 'dp'), may hold values from -0.109375 to 0.109375
- sample_ids: int32 [16384], P(('dp', 'mp')), may hold values from 0 to 127, as said below
- variate_ids: int32 [16384], P(('dp', 'mp')), may hold values from 0 to 15, as said below
- time_ids: int32 [16384], P(('dp', 'mp')), may hold values from 0 to 31, as said below
Outputs:
- encoded: bfloat16 [16384, 1024], P(('dp', 'mp'))
Inputs may be any that keep to these rules, and one draw needn't show every extreme that they name: `sample_ids`: within each packed sequence of 512 tokens the series numbers start at 0 and never fall; a series with v variates (1 to 16) and p patches (4 to 32) holds v * p consecutive tokens, the last series of a sequence may be cut short; some packed sequence holds 128 series of one variate and four patches each. `variate_ids`: A token's offset within its series divided by that series' patch count p. `time_ids`: A token's offset within its series modulo that series' patch count p.
All inputs are finite; a program needn't handle non-finite values.
Results may differ from a plain program's by a relative error of at most 0.017.
Values may be sent and summed in bfloat16 or wider, within the bound.
A program may use at most 128 MiB of HBM per device.

v0:
```python
import jax
import jax.numpy as jnp
from jax import lax
from jax.sharding import PartitionSpec as P

HEAD_DIM = 64
L = 512


def rms_norm(values, gain):
    wide = values.astype(jnp.float32)
    square = jnp.mean(wide * wide, axis=-1, keepdims=True)
    return (wide * lax.rsqrt(square + 1e-05) * gain[None, :]).astype(jnp.bfloat16)


def rotate(values, times):
    half = values.shape[-1] // 2
    freq = 10000.0 ** (-jnp.arange(half, dtype=jnp.float32) / half)
    angle = times.astype(jnp.float32)[:, None] * freq[None, :]
    cosine = jnp.cos(angle)[:, None, :]
    sine = jnp.sin(angle)[:, None, :]
    first = values[..., :half]
    second = values[..., half:]
    return jnp.concatenate(
        [first * cosine - second * sine, first * sine + second * cosine], axis=-1
    )


def rotated(raw, times):
    row_total, local_width = raw.shape
    turned = rotate(raw.reshape(row_total, local_width // HEAD_DIM, HEAD_DIM), times)
    return turned.reshape(row_total, local_width).astype(jnp.bfloat16)


def attend(queries, keys_rot, values, samples, variates, bias):
    row_total, local_width = queries.shape
    heads_here = local_width // HEAD_DIM
    count = row_total // L

    def one_sequence(args):
        qs, ks, vs, sample_row, variate_row = args
        scores = jnp.einsum(
            "qhd,khd->hqk", qs, ks, preferred_element_type=jnp.float32
        ) * HEAD_DIM ** (-0.5)
        same = variate_row[:, None] == variate_row[None, :]
        scores = scores + jnp.where(same[None], bias[0][:, None, None], bias[1][:, None, None])
        scores = jnp.where((sample_row[:, None] == sample_row[None, :])[None], scores, -1e30)
        top = jnp.max(scores, axis=2, keepdims=True)
        expo = jnp.exp(scores - top)
        weights = (expo / jnp.sum(expo, axis=2, keepdims=True)).astype(jnp.bfloat16)
        return jnp.einsum("hqk,khd->qhd", weights, vs, preferred_element_type=jnp.float32).astype(
            jnp.bfloat16
        )

    shape = (count, L, heads_here, HEAD_DIM)
    result = lax.map(
        one_sequence,
        (
            queries.reshape(shape),
            keys_rot.reshape(shape),
            values.reshape(shape),
            samples.reshape(count, L),
            variates.reshape(count, L),
        ),
    )
    return result.reshape(row_total, local_width)


def local(
    tokens,
    norm_gain,
    qkv_weight,
    out_weight,
    variate_bias,
    ffn_weight,
    down_weight,
    sample_ids,
    variate_ids,
    time_ids,
):
    first_normed = rms_norm(tokens, norm_gain[0])
    wide_columns = lax.all_gather(qkv_weight, "mp", axis=2, tiled=True)
    columns = first_normed
    projected = jnp.einsum(
        "rc,jcd->jrd",
        columns,
        lax.all_gather(wide_columns, "dp", axis=1, tiled=True),
        preferred_element_type=jnp.float32,
    )
    queries = rotated(projected[0], time_ids)
    keys_rot = rotated(projected[1], time_ids)
    values = projected[2].astype(jnp.bfloat16)
    back_rows = attend(queries, keys_rot, values, sample_ids, variate_ids, variate_bias)
    out_rows = lax.all_gather(out_weight, "mp", axis=0, tiled=True)
    mixed = jnp.dot(
        back_rows,
        lax.all_gather(out_rows, "dp", axis=1, tiled=True),
        preferred_element_type=jnp.float32,
    )
    residual = (tokens.astype(jnp.float32) + mixed).astype(jnp.bfloat16)
    second_normed = rms_norm(residual, norm_gain[1])
    ffn_columns = lax.all_gather(ffn_weight, "mp", axis=2, tiled=True)
    columns = second_normed
    gate_up = jnp.einsum(
        "rc,jcf->jrf",
        columns,
        lax.all_gather(ffn_columns, "dp", axis=1, tiled=True),
        preferred_element_type=jnp.float32,
    )
    hidden = (jax.nn.silu(gate_up[0]) * gate_up[1]).astype(jnp.bfloat16)
    down_full = lax.all_gather(down_weight, "mp", axis=0, tiled=True)
    feed = jnp.dot(
        hidden,
        lax.all_gather(down_full, "dp", axis=1, tiled=True),
        preferred_element_type=jnp.float32,
    )
    return (residual.astype(jnp.float32) + feed).astype(jnp.bfloat16)


def solution(mesh):
    return jax.shard_map(
        local,
        mesh=mesh,
        in_specs=(
            P(("dp", "mp"), None),
            P(),
            P(None, "dp", "mp"),
            P("mp", "dp"),
            P(),
            P(None, "dp", "mp"),
            P("mp", "dp"),
            P(("dp", "mp")),
            P(("dp", "mp")),
            P(("dp", "mp")),
        ),
        out_specs=P(("dp", "mp"), None),
        check_vma=False,
    )
```

profile of v0, /device:TPU:0, one launch (start us, length us, event | category | flops | bytes accessed | tf_op | source)
XLA Modules:
  0.0 265.7 jit_solution(9024680529559725444)
XLA Ops:
  6.6 2.2 copy.27
  8.9 27.7 %all_gather.24 = bf16[3,128,1024]{2,1,0:T(8,128)(2,1)} all-gather(bf16[3,128,256]{2,1,0:T(8,128)(2,1)} %param.12), channel_id=1, replica_groups=mesh['dp'=8,'mp'=4] {'mp'}, dimensions={2}, use_global_device_ids=true | all-gather | bytes 983040 | tf_op jit(solution)/shard_map/all_gather | solution.py:82
  36.7 19.0 %all_gather.26 = bf16[1024,128]{1,0:T(8,128)(2,1)} all-gather(bf16[256,128]{1,0:T(8,128)(2,1)} %param.13), channel_id=1, replica_groups=mesh['dp'=8,'mp'=4] {'mp'}, dimensions={0}, use_global_device_ids=true | all-gather | bytes 327680 | tf_op jit(solution)/shard_map/all_gather | solution.py:94
  55.7 1.1 all-gather.10.cloned.1.call-done
  56.9 4.9 %copy.28 = bf16[2,128,2816]{2,1,0:T(8,128)(2,1)} copy(bf16[2,128,2816]{1,0,2:T(2,128)(2,1)} %all-gather.10.cloned.1.call-done) | data formatting | bytes 2883584 | tf_op jit(solution)/shard_map/all_gather | solution.py:102
  61.8 18.1 %all_gather.30 = bf16[2816,128]{1,0:T(8,128)(2,1)} all-gather(bf16[704,128]{1,0:T(8,128)(2,1)S(1)} %copy-done.3), channel_id=1, replica_groups=mesh['dp'=8,'mp'=4] {'mp'}, dimensions={0}, use_global_device_ids=true | all-gather | bytes 901120 | tf_op jit(solution)/shard_map/all_gather | solution.py:111
  80.0 0.3 fusion.15
  80.3 0.3 multiply_cosine_fusion
  80.6 1.1 broadcast_compare_fusion
  81.7 21.9 %all-gather.6.cloned.1.call-done = bf16[3,1024,1024]{2,1,0:T(8,128)(2,1)} async-done(((bf16[3,128,1024]{2,1,0:T(8,128)(2,1)}), bf16[3,1024,1024]{2,1,0:T(8,128)(2,1)}) %all-gather.6.cloned.1.call-update) | async-done | bytes 6291472 | tf_op jit(solution)/shard_map/all_gather | solution.py:87
  103.6 5.7 %convolution_bitcast_fusion.1 = f32[3,512,1024]{2,1,0:T(8,128)S(1)} fusion(bf16[3,1024,1024]{2,1,0:T(8,128)(2,1)} %all-gather.6.cloned.1.call-done, bf16[512,1024]{1,0:T(8,128)(2,1)S(1)} %copy-done, f32[1024]{0:T(1024)S(1)} %bitcast.48, f32[512]{0:T(512)S(1)} %add_rsqrt_fusion.1), kind=kOutput, calls=%fused_computation.25 | convolution fusion | flops 3223322624 | bytes 13637632 | tf_op jit(solution)/shard_map/rc,jcd->jrd/dot_general | solution.py:84
  109.3 0.2 slice.89
  109.4 2.4 fusion.49
  111.9 2.0 copy.24
  113.8 2.9 %copy.25 = f32[1,512,1024]{1,2,0:T(8,128)} copy(f32[1,512,1024]{2,1,0:T(8,128)} %get-tuple-element.20) | data formatting | bytes 4194304 | tf_op jit(solution)/shard_map/slice | solution.py:91
  116.8 1.3 copy.23
  118.1 3.2 %subtract_convert_fusion.1 = (bf16[512,16,32]{0,2,1:T(8,128)(2,1)S(1)}, bf16[512,16,32]{0,2,1:T(8,128)(2,1)S(1)}, bf16[512,16,32]{0,2,1:T(8,128)(2,1)}, bf16[512,16,32]{0,2,1:T(8,128)(2,1)}) fusion(f32[512,16,64]{0,2,1:T(8,128)S(1)} %bitcast.44, f32[512,32]{0,1:T(8,128)S(1)} %get-tuple-element.40, f32[512,32]{0,1:T(8,128)S(1)} %get-tuple-element.39, ...), kind=kLoop, calls=%fused_computation.45 | loop fusion | flops 4194304 | bytes 6422528 | tf_op jit(solution)/shard_map/convert.2
  121.3 9.0 %fusion.51 = f32[16,512]{1,0:T(8,128)S(1)} fusion(f32[16]{0:T(128)S(1)} %get-tuple-element.42, f32[16]{0:T(128)S(1)} %get-tuple-element.41, pred[512,512]{0,1:T(8,128)(4,1)S(1)} %get-tuple-element.45, pred[512,512]{0,1:T(8,128)(4,1)} %get-tuple-element.46, bf16[512,16,32]{0,2,1:T(8,128)(2,1)} %get-tuple-element.34, ...), kind=kOutput, calls=%fused_computation.69 | convolution fusion | flops 566231552 | bytes 2654336 | tf_op jit(solution)/shard_map/while/body/eval_jaxpr/sub | solution.py:49
  130.3 11.1 %fusion.25 = bf16[16,64,512]{2,1,0:T(8,128)(2,1)} fusion(bf16[512,16,64]{0,2,1:T(8,128)(2,1)S(1)} %bitcast.46, f32[16,512]{1,0:T(8,128)S(1)} %fusion.51, f32[16]{0:T(128)S(1)} %get-tuple-element.42, f32[16]{0:T(128)S(1)} %get-tuple-element.41, pred[512,512]{0,1:T(8,128)(4,1)S(1)} %get-tuple-element.45, pred[512,512]{0,1:T(8,128)(4,1)} %get-tuple-element.46, ...), kind=kOutput, calls=%fused_computation.35 | convolution fusion | flops 1107829248 | bytes 4751488 | tf_op jit(solution)/shard_map/while/body/eval_jaxpr/hqk,khd->qhd/dot_general | solution.py:51
  141.4 3.8 %fusion.19 = (f32[512]{0:T(512)S(1)}, bf16[512,1024]{1,0:T(8,128)(2,1)S(1)}) fusion(bf16[512,1024]{0,1:T(8,128)(2,1)} %bitcast.49, bf16[1024,1024]{1,0:T(8,128)(2,1)} %all-gather.8.cloned.1.call-done, bf16[512,1024]{1,0:T(8,128)(2,1)S(1)} %copy-done.1), kind=kOutput, calls=%fused_computation.30 | convolution fusion | flops 1076887040 | bytes 5244928 | tf_op jit(solution)/shard_map/dot_general | solution.py:95
  145.2 57.8 %all-gather.12.cloned.1.call-done = bf16[2,1024,2816]{2,1,0:T(8,128)(2,1)} async-done(((bf16[2,128,2816]{2,1,0:T(8,128)(2,1)}), bf16[2,1024,2816]{2,1,0:T(8,128)(2,1)}) %all-gather.12.cloned.1.call-update) | async-done | bytes 11534352 | tf_op jit(solution)/shard_map/all_gather | solution.py:107
  202.9 13.3 %convolution_bitcast_fusion = f32[2,512,2816]{2,1,0:T(8,128)} fusion(bf16[2,1024,2816]{2,1,0:T(8,128)(2,1)} %all-gather.12.cloned.1.call-done, bf16[512,1024]{1,0:T(8,128)(2,1)S(1)} %get-tuple-element.44, f32[1024]{0:T(1024)S(1)} %bitcast.47, f32[512]{0:T(512)S(1)} %add_rsqrt_fusion), kind=kOutput, calls=%fused_computation.12 | convolution fusion | flops 5907677184 | bytes 24123392 | tf_op jit(solution)/shard_map/rc,jcf->jrf/dot_general | solution.py:104
  216.2 32.7 %all-gather.14.cloned.1.call-done = bf16[2816,1024]{1,0:T(8,128)(2,1)} async-done(((bf16[2816,128]{1,0:T(8,128)(2,1)}), bf16[2816,1024]{1,0:T(8,128)(2,1)}) %all-gather.14.cloned.1.call-update) | async-done | bytes 5767184 | tf_op jit(solution)/shard_map/all_gather | solution.py:114
  249.0 10.2 %fusion.22 = bf16[512,1024]{1,0:T(8,128)(2,1)} fusion(bf16[512,1024]{1,0:T(8,128)(2,1)S(1)} %get-tuple-element.44, bf16[2816,1024]{1,0:T(8,128)(2,1)} %all-gather.14.cloned.1.call-done, f32[2,512,2816]{2,1,0:T(8,128)} %convolution_bitcast_fusion), kind=kOutput, calls=%fused_computation.33 | convolution fusion | flops 2963013632 | bytes 19398656 | tf_op jit(solution)/shard_map/dot_general | solution.py:112
  (35 shorter events, 0.4 us)
Async XLA Ops:
  6.5 55.3 %copy-start.3 = (bf16[704,128]{1,0:T(8,128)(2,1)S(1)}, bf16[704,128]{1,0:T(8,128)(2,1)}, u32[]{:S(2)}) copy-start(bf16[704,128]{1,0:T(8,128)(2,1)} %param.16) | copy-start | bytes 540676
  6.5 73.4 %copy-start.7 = (s32[512]{0:T(512)S(1)}, s32[512]{0:T(512)}, u32[]{:S(2)}) copy-start(s32[512]{0:T(512)} %param.19) | copy-start | bytes 6148
  6.5 73.4 %copy-start = (bf16[512,1024]{1,0:T(8,128)(2,1)S(1)}, bf16[512,1024]{1,0:T(8,128)(2,1)}, u32[]{:S(2)}) copy-start(bf16[512,1024]{1,0:T(8,128)(2,1)} %param.10) | copy-start | bytes 3145732
  6.5 73.7 %copy-start.8 = (f32[2,16]{1,0:T(2,128)S(1)}, f32[2,16]{1,0:T(2,128)}, u32[]{:S(2)}) copy-start(f32[2,16]{1,0:T(2,128)} %param.14) | copy-start | bytes 388
  6.5 73.7 %copy-start.6 = (f32[2,1024]{1,0:T(2,128)S(1)}, f32[2,1024]{1,0:T(2,128)}, u32[]{:S(2)}) copy-start(f32[2,1024]{1,0:T(2,128)} %param.11) | copy-start | bytes 24580
  6.5 74.1 %copy-start.5 = (s32[512]{0:T(512)S(1)}, s32[512]{0:T(512)}, u32[]{:S(2)}) copy-start(s32[512]{0:T(512)} %param.17) | copy-start | bytes 6148
  6.6 74.1 %copy-start.4 = (s32[512]{0:T(512)S(1)}, s32[512]{0:T(512)}, u32[]{:S(2)}) copy-start(s32[512]{0:T(512)} %param.18) | copy-start | bytes 6148
  6.6 50.3 %all-gather.10.cloned.1.call-start = ((), (), s32[]{:S(2)}) async-start(), calls=%async_computation.2 | async-start | bytes 1802240 | tf_op jit(solution)/shard_map/all_gather | solution.py:102
  8.8 94.8 %all-gather.6.cloned.1.call-start = ((), (), s32[]{:S(2)}) async-start(), calls=%async_computation | async-start | bytes 7077888 | tf_op jit(solution)/shard_map/all_gather | solution.py:87
  36.6 104.8 %all-gather.8.cloned.1.call-start = ((), (), s32[]{:S(2)}) async-start(), calls=%async_computation.1 | async-start | bytes 2359296 | tf_op jit(solution)/shard_map/all_gather | solution.py:97
  55.7 147.3 %all-gather.12.cloned.1.call-start = ((), (), s32[]{:S(2)}) async-start(), calls=%async_computation.3 | async-start | bytes 12976128 | tf_op jit(solution)/shard_map/all_gather | solution.py:107
  61.8 187.2 %all-gather.14.cloned.1.call-start = ((), (), s32[]{:S(2)}) async-start(), calls=%async_computation.4 | async-start | bytes 6488064 | tf_op jit(solution)/shard_map/all_gather | solution.py:114
  121.3 9.0 %copy-start.2 = (bf16[1,512,1024]{1,2,0:T(8,128)(2,1)S(1)}, bf16[1,512,1024]{1,2,0:T(8,128)(2,1)}, u32[]{:S(2)}) copy-start(bf16[1,512,1024]{1,2,0:T(8,128)(2,1)} %copy.23) | copy-start | bytes 3145732
  130.3 11.1 %copy-start.1 = (bf16[512,1024]{1,0:T(8,128)(2,1)S(1)}, bf16[512,1024]{1,0:T(8,128)(2,1)}, u32[]{:S(2)}) copy-start(bf16[512,1024]{1,0:T(8,128)(2,1)} %param.10) | copy-start | bytes 3145732
Sparse Core Ops, SparseCore 0:
  8.9 47.8 all-gather.9
  58.8 44.7 all-gather.5
  105.5 28.0 all-gather.7
  135.4 67.5 all-gather.11
  204.7 44.2 all-gather.13
where the time goes:
time: 266 us
  waiting for transfers between devices  114 us (43%)
  blocking collectives  64.8 us (24%)
  matrix products  53 us (20%)
  local copies, waits for them, and re-layouts  15.9 us (6%)
  between operations  13.3 us (5%)
  other arithmetic  4.88 us (2%)
    all_gather x1, waiting for transfers between devices, local(): lax.all_gather(ffn_columns, 'dp', axis=1, tiled=True)  57.8 us
    all_gather x1, waiting for transfers between devices, local(): lax.all_gather(down_full, 'dp', axis=1, tiled=True)  32.7 us
    all_gather x1, blocking collectives, local(): wide_columns = lax.all_gather(qkv_weight, 'mp', axis=2, tiled=True)  27.7 us
    all_gather x1, waiting for transfers between devices, local(): lax.all_gather(wide_columns, 'dp', axis=1, tiled=True)  21.9 us
    all_gather x1, blocking collectives, local(): out_rows = lax.all_gather(out_weight, 'mp', axis=0, tiled=True)  19 us
    all_gather x1, blocking collectives, local(): down_full = lax.all_gather(down_weight, 'mp', axis=0, tiled=True)  18.1 us
    dot_general x1, matrix products, local(): jnp.einsum('rc,jcf->jrf', columns, lax.all_gather(ffn_columns, 'dp', axis...  13.3 us
    dot_general x1, matrix products, one_sequence(): jnp.einsum('hqk,khd->qhd', weights, vs, preferred_element_type=jnp.float32)  11.1 us
  transfers between devices with their start and end apart: 5, of which 4 were waited for; matrix products, arithmetic and copies ran while one was open for 23% of the time, Pallas kernels for 0%

commit v1 on v0

--- a/solution.py
+++ b/solution.py
@@ -101,12 +101,37 @@
     second_normed = rms_norm(residual, norm_gain[1])
     ffn_columns = lax.all_gather(ffn_weight, "mp", axis=2, tiled=True)
     columns = second_normed
+    size, here, rows = (lax.axis_size("dp"), lax.axis_index("dp"), ffn_columns.shape[1])
+    ahead = [(i, (i + 1) % size) for i in range(size)]
+    left = [(i, (i - 1) % size) for i in range(size)]
+    middle = size // 2
+    from_left = from_right = ffn_columns
     gate_up = jnp.einsum(
         "rc,jcf->jrf",
-        columns,
-        lax.all_gather(ffn_columns, "dp", axis=1, tiled=True),
+        lax.dynamic_slice_in_dim(columns, here * rows, ffn_columns.shape[1], axis=1),
+        ffn_columns,
         preferred_element_type=jnp.float32,
     )
+    for step in range(1, middle + 1):
+        from_left = lax.ppermute(from_left, "dp", ahead)
+        if step < size - middle:
+            from_right = lax.ppermute(from_right, "dp", left)
+            gate_up = gate_up + jnp.einsum(
+                "rc,jcf->jrf",
+                lax.dynamic_slice_in_dim(
+                    columns, (here + step) % size * rows, from_right.shape[1], axis=1
+                ),
+                from_right,
+                preferred_element_type=jnp.float32,
+            )
+        gate_up = gate_up + jnp.einsum(
+            "rc,jcf->jrf",
+            lax.dynamic_slice_in_dim(
+                columns, (here - step) % size * rows, from_left.shape[1], axis=1
+            ),
+            from_left,
+            preferred_element_type=jnp.float32,
+        )
     hidden = (jax.nn.silu(gate_up[0]) * gate_up[1]).astype(jnp.bfloat16)
     down_full = lax.all_gather(down_weight, "mp", axis=0, tiled=True)
     feed = jnp.dot(

time: 266 us -> 308 us (1.16)
  matrix products: 53 us -> 117 us
  waiting for transfers between devices: 114 us -> 91.2 us
  local copies, waits for them, and re-layouts: 15.9 us -> 9.76 us
  starting transfers between devices: 0.21 us -> 6.28 us
    ppermute x0 -> x7, waiting for transfers between devices: none -> 87.7 us  [the longest x4 83.6 us: local(): from_left = lax.ppermute(from_left, 'dp', ahead)]
    dot_general x1 -> x8, matrix products: 13.3 us -> 76.5 us  [the longest x4 50.1 us: local(): jnp.einsum('rc,jcf->jrf', lax.dynamic_slice_in_dim(columns, (here - step)...]
    all_gather x1 -> x0, waiting for transfers between devices: 57.8 us -> none  [local(): lax.all_gather(ffn_columns, 'dp', axis=1, tiled=True)]
    all_gather x1, waiting for transfers between devices: 32.7 us -> 0.01 us  [local(): lax.all_gather(down_full, 'dp', axis=1, tiled=True)]
    all_gather x1, waiting for transfers between devices: 21.9 us -> 0.01 us  [local(): lax.all_gather(wide_columns, 'dp', axis=1, tiled=True)]
    ppermute x0 -> x7, starting transfers between devices: none -> 6.12 us  [the longest x3 6.1 us: local(): from_right = lax.ppermute(from_right, 'dp', left)]
    all_gather x1 -> x0, local copies, waits for them, and re-layouts: 4.91 us -> none  [local(): ffn_columns = lax.all_gather(ffn_weight, 'mp', axis=2, tiled=True)]
  transfers between devices with their start and end apart: 5 -> 11, of which waited for: 4 -> 5; matrix products, arithmetic and copies ran while one was open for 23% -> 40% of each run, Pallas kernels for 0% -> 0%
where the time goes in v1:
time: 308 us; the launch traced here: 307 us
  matrix products  117 us (38%)
  waiting for transfers between devices  91.2 us (30%)
  blocking collectives  63.4 us (21%)
  between operations  13.5 us (4%)
  local copies, waits for them, and re-layouts  9.76 us (3%)
  other arithmetic  6.35 us (2%)
  starting transfers between devices  6.28 us (2%)
    ppermute x4, waiting for transfers between devices, local(): from_left = lax.ppermute(from_left, 'dp', ahead)  83.6 us
    dot_general x4, matrix products, local(): jnp.einsum('rc,jcf->jrf', lax.dynamic_slice_in_dim(columns, (here - step)...  50.1 us
    all_gather x1, blocking collectives, local(): wide_columns = lax.all_gather(qkv_weight, 'mp', axis=2, tiled=True)  26.3 us
    dot_general x3, matrix products, local(): jnp.einsum('rc,jcf->jrf', lax.dynamic_slice_in_dim(columns, (here + step)...  20.6 us
    all_gather x1, blocking collectives, local(): out_rows = lax.all_gather(out_weight, 'mp', axis=0, tiled=True)  18.8 us
    all_gather x1, blocking collectives, local(): down_full = lax.all_gather(down_weight, 'mp', axis=0, tiled=True)  18.3 us
    dot_general x1, matrix products, one_sequence(): jnp.einsum('hqk,khd->qhd', weights, vs, preferred_element_type=jnp.float32)  11.1 us
    dot_general x1, matrix products, local(): jnp.dot(hidden, lax.all_gather(down_full, 'dp', axis=1, tiled=True), pref...  10.2 us
  transfers between devices with their start and end apart: 11, of which 5 were waited for; matrix products, arithmetic and copies ran while one was open for 40% of the time, Pallas kernels for 0%

profile of v1, /device:TPU:0, one launch (start us, length us, event | category | flops | bytes accessed | tf_op | source)
XLA Modules:
  0.0 307.1 jit_solution(17564873382233900211)
XLA Ops:
  7.3 26.3 %all_gather.21 = bf16[3,128,1024]{2,1,0:T(8,128)(2,1)} all-gather(bf16[3,128,256]{2,1,0:T(8,128)(2,1)} %param.12), channel_id=1, replica_groups=mesh['dp'=8,'mp'=4] {'mp'}, dimensions={2}, use_global_device_ids=true | all-gather | bytes 983040 | tf_op jit(solution)/shard_map/all_gather | solution.py:82
  33.7 18.8 %all_gather.23 = bf16[1024,128]{1,0:T(8,128)(2,1)} all-gather(bf16[256,128]{1,0:T(8,128)(2,1)} %param.13), channel_id=1, replica_groups=mesh['dp'=8,'mp'=4] {'mp'}, dimensions={0}, use_global_device_ids=true | all-gather | bytes 327680 | tf_op jit(solution)/shard_map/all_gather | solution.py:94
  52.6 2.8 all-gather.9.cloned.1.call-done
  55.4 2.6 collective-permute-start
  58.0 43.2 %collective-permute-done.1 = bf16[2,128,2816]{1,2,0:T(8,128)(2,1)S(1)} collective-permute-done((bf16[2,128,2816]{1,2,0:T(8,128)(2,1)}, bf16[2,128,2816]{1,2,0:T(8,128)(2,1)S(1)}, u32[]{:S(2)}, u32[]{:S(2)}) %collective-permute-start.1) | collective-permute-done | bytes 1441824 | tf_op jit(solution)/shard_map/ppermute | solution.py:116
  102.3 4.0 %collective-permute-done = bf16[2,128,2816]{1,2,0:T(8,128)(2,1)S(1)} collective-permute-done((bf16[2,128,2816]{1,2,0:T(8,128)(2,1)}, bf16[2,128,2816]{1,2,0:T(8,128)(2,1)S(1)}, u32[]{:S(2)}, u32[]{:S(2)}) %collective-permute-start) | collective-permute-done | bytes 1441824 | tf_op jit(solution)/shard_map/ppermute | solution.py:118
  106.4 2.8 collective-permute-start.2
  109.1 38.9 %collective-permute-done.3 = bf16[2,128,2816]{1,2,0:T(8,128)(2,1)S(1)} collective-permute-done((bf16[2,128,2816]{1,2,0:T(8,128)(2,1)S(1)}, bf16[2,128,2816]{1,2,0:T(8,128)(2,1)S(1)}, u32[]{:S(2)}, u32[]{:S(2)}) %collective-permute-start.3) | collective-permute-done | bytes 1441824 | tf_op jit(solution)/shard_map/ppermute | solution.py:116
  148.1 18.3 %all_gather.26 = bf16[2816,128]{1,0:T(8,128)(2,1)} all-gather(bf16[704,128]{1,0:T(8,128)(2,1)} %param.16), channel_id=1, replica_groups=mesh['dp'=8,'mp'=4] {'mp'}, dimensions={0}, use_global_device_ids=true | all-gather | bytes 901120 | tf_op jit(solution)/shard_map/all_gather | solution.py:136
  171.8 6.3 %convolution_bitcast_fusion = f32[3,512,1024]{2,1,0:T(8,128)S(1)} fusion(bf16[3,1024,1024]{2,1,0:T(8,128)(2,1)} %all-gather.5.cloned.1.call-done, bf16[512,1024]{1,0:T(8,128)(2,1)} %param.10, f32[1024]{0:T(1024)S(1)} %bitcast.76, f32[512]{0:T(512)S(1)} %add_rsqrt_fusion.1), kind=kOutput, calls=%fused_computation.25 | convolution fusion | flops 3223322624 | bytes 13637632 | tf_op jit(solution)/shard_map/rc,jcd->jrd/dot_general | solution.py:84
  182.4 2.9 copy.26
  186.7 3.2 %subtract_convert_fusion.1 = (bf16[512,16,32]{0,2,1:T(8,128)(2,1)S(1)}, bf16[512,16,32]{0,2,1:T(8,128)(2,1)S(1)}, bf16[512,16,32]{0,2,1:T(8,128)(2,1)}, bf16[512,16,32]{0,2,1:T(8,128)(2,1)}) fusion(f32[512,16,64]{0,2,1:T(8,128)S(1)} %bitcast.72, f32[512,32]{0,1:T(8,128)S(1)} %get-tuple-element.40, f32[512,32]{0,1:T(8,128)S(1)} %get-tuple-element.39, ...), kind=kLoop, calls=%fused_computation.42 | loop fusion | flops 4194304 | bytes 6422528 | tf_op jit(solution)/shard_map/convert.2
  189.8 9.0 %fusion.78 = f32[16,512]{1,0:T(8,128)S(1)} fusion(f32[16]{0:T(128)S(1)} %get-tuple-element.42, f32[16]{0:T(128)S(1)} %get-tuple-element.41, pred[512,512]{0,1:T(8,128)(4,1)S(1)} %get-tuple-element.45, pred[512,512]{0,1:T(8,128)(4,1)} %get-tuple-element.46, bf16[512,16,32]{0,2,1:T(8,128)(2,1)} %get-tuple-element.34, ...), kind=kOutput, calls=%fused_computation.97 | convolution fusion | flops 566231552 | bytes 2654336 | tf_op jit(solution)/shard_map/while/body/eval_jaxpr/sub | solution.py:49
  198.9 11.1 %fusion.25 = bf16[16,64,512]{2,1,0:T(8,128)(2,1)} fusion(bf16[512,16,64]{0,2,1:T(8,128)(2,1)S(1)} %bitcast.74, f32[16,512]{1,0:T(8,128)S(1)} %fusion.78, f32[16]{0:T(128)S(1)} %get-tuple-element.42, f32[16]{0:T(128)S(1)} %get-tuple-element.41, pred[512,512]{0,1:T(8,128)(4,1)S(1)} %get-tuple-element.45, pred[512,512]{0,1:T(8,128)(4,1)} %get-tuple-element.46, ...), kind=kOutput, calls=%fused_computation.35 | convolution fusion | flops 1107829248 | bytes 4751488 | tf_op jit(solution)/shard_map/while/body/eval_jaxpr/hqk,khd->qhd/dot_general | solution.py:51
  210.0 3.5 %fusion.19 = (f32[512]{0:T(512)S(1)}, bf16[512,1024]{1,0:T(8,128)(2,1)S(1)}) fusion(bf16[512,1024]{0,1:T(8,128)(2,1)} %bitcast.77, bf16[1024,1024]{1,0:T(8,128)(2,1)} %all-gather.7.cloned.1.call-done, bf16[512,1024]{1,0:T(8,128)(2,1)S(1)} %copy-done.7), kind=kOutput, calls=%fused_computation.30 | convolution fusion | flops 1076887040 | bytes 5244928 | tf_op jit(solution)/shard_map/dot_general | solution.py:95
  213.8 6.0 %fusion.36 = f32[512,2,2816]{2,0,1:T(8,128)} fusion(bf16[2,128,2816]{1,2,0:T(8,128)(2,1)S(1)} %copy-done.6, bf16[512,1024]{1,0:T(8,128)(2,1)S(1)} %fusion.21, s32[]{:T(128)S(6)} %select_n.75), kind=kOutput, calls=%fused_computation.53 | convolution fusion | flops 738197504 | bytes 13107204 | tf_op jit(solution)/shard_map/rc,jcf->jrf/dot_general | solution.py:127
  219.8 7.6 %fusion.38 = f32[512,2,2816]{2,0,1:T(8,128)} fusion(bf16[2,128,2816]{1,2,0:T(8,128)(2,1)} %collective-permute-done.2, bf16[512,1024]{1,0:T(8,128)(2,1)S(1)} %fusion.21, s32[]{:T(128)S(6)} %select_n.73), kind=kOutput, calls=%fused_computation.55 | convolution fusion | flops 738197504 | bytes 13107204 | tf_op jit(solution)/shard_map/rc,jcf->jrf/dot_general | solution.py:119
  227.4 5.9 %fusion.40 = f32[512,2,2816]{2,0,1:T(8,128)} fusion(bf16[2,128,2816]{1,2,0:T(8,128)(2,1)S(1)} %copy-done.2, bf16[512,1024]{1,0:T(8,128)(2,1)S(1)} %fusion.21, s32[]{:T(128)S(6)} %select_n.71), kind=kOutput, calls=%fused_computation.57 | convolution fusion | flops 738197504 | bytes 13107204 | tf_op jit(solution)/shard_map/rc,jcf->jrf/dot_general | solution.py:127
  233.3 5.8 %fusion.42 = f32[512,2,2816]{2,0,1:T(8,128)} fusion(bf16[2,128,2816]{1,2,0:T(8,128)(2,1)S(1)} %copy-done.4, bf16[512,1024]{1,0:T(8,128)(2,1)S(1)} %fusion.21, s32[]{:T(128)S(6)} %select_n.69), kind=kOutput, calls=%fused_computation.59 | convolution fusion | flops 738197504 | bytes 13107204 | tf_op jit(solution)/shard_map/rc,jcf->jrf/dot_general | solution.py:119
  239.1 7.5 %fusion.32 = f32[512,2,2816]{2,0,1:T(8,128)} fusion(bf16[2,128,2816]{1,2,0:T(8,128)(2,1)} %collective-permute-done.5, bf16[512,1024]{1,0:T(8,128)(2,1)S(1)} %fusion.21, s32[]{:T(128)S(6)} %select_n.79), kind=kOutput, calls=%fused_computation.49 | convolution fusion | flops 738197504 | bytes 13107204 | tf_op jit(solution)/shard_map/rc,jcf->jrf/dot_general | solution.py:127
  246.6 5.8 %fusion.44 = f32[512,2,2816]{2,0,1:T(8,128)} fusion(bf16[2,128,2816]{1,2,0:T(8,128)(2,1)S(1)} %copy-done, bf16[512,1024]{1,0:T(8,128)(2,1)S(1)} %fusion.21, s32[]{:T(128)S(6)} %select_n.67), kind=kOutput, calls=%fused_computation.61 | convolution fusion | flops 738197504 | bytes 13107204 | tf_op jit(solution)/shard_map/rc,jcf->jrf/dot_general | solution.py:109
  252.5 7.2 %fusion.34 = f32[512,2,2816]{2,0,1:T(8,128)} fusion(bf16[2,128,2816]{1,2,0:T(8,128)(2,1)} %collective-permute-done.4, bf16[512,1024]{1,0:T(8,128)(2,1)S(1)} %fusion.21, s32[]{:T(128)S(6)} %select_n.77), kind=kOutput, calls=%fused_computation.51 | convolution fusion | flops 738197504 | bytes 13107204 | tf_op jit(solution)/shard_map/rc,jcf->jrf/dot_general | solution.py:119
  259.7 30.7 %add_bitcast_fusion = f32[2,512,2816]{2,1,0:T(8,128)} fusion(f32[512,2,2816]{2,0,1:T(8,128)} %fusion.32, f32[512,2,2816]{2,0,1:T(8,128)} %fusion.34, f32[512,2,2816]{2,0,1:T(8,128)} %fusion.36, f32[512,2,2816]{2,0,1:T(8,128)} %fusion.38, f32[512,2,2816]{2,0,1:T(8,128)} %fusion.40, f32[512,2,2816]{2,0,1:T(8,128)} %fusion.44, f32[512,2,2816]{2,0,1:T(8,128)} %fusion.42, ...), kind=kOutput, calls=%fused_computation.5 | convolution fusion | flops 758382592 | bytes 93847552 | tf_op jit(solution)/shard_map/rc,jcf->jrf/dot_general | solution.py:127
  290.3 10.2 %fusion.22 = bf16[512,1024]{1,0:T(8,128)(2,1)} fusion(bf16[512,1024]{1,0:T(8,128)(2,1)S(1)} %get-tuple-element.44, bf16[2816,1024]{1,0:T(8,128)(2,1)} %all-gather.11.cloned.1.call-done, f32[2,512,2816]{2,1,0:T(8,128)} %add_bitcast_fusion), kind=kOutput, calls=%fused_computation.33 | convolution fusion | flops 2963013632 | bytes 19398656 | tf_op jit(solution)/shard_map/dot_general | solution.py:137
  (62 shorter events, 13.2 us)
Async XLA Ops:
  6.5 160.0 %copy-start.12 = (s32[512]{0:T(512)S(1)}, s32[512]{0:T(512)}, u32[]{:S(2)}) copy-start(s32[512]{0:T(512)} %param.19) | copy-start | bytes 6148
  6.5 161.6 %copy-start.13 = (f32[2,16]{1,0:T(2,128)S(1)}, f32[2,16]{1,0:T(2,128)}, u32[]{:S(2)}) copy-start(f32[2,16]{1,0:T(2,128)} %param.14) | copy-start | bytes 388
  6.5 161.6 %copy-start.11 = (f32[2,1024]{1,0:T(2,128)S(1)}, f32[2,1024]{1,0:T(2,128)}, u32[]{:S(2)}) copy-start(f32[2,1024]{1,0:T(2,128)} %param.11) | copy-start | bytes 24580
  6.5 161.9 %copy-start.10 = (s32[512]{0:T(512)S(1)}, s32[512]{0:T(512)}, u32[]{:S(2)}) copy-start(s32[512]{0:T(512)} %param.17) | copy-start | bytes 6148
  6.5 161.9 %copy-start.9 = (s32[512]{0:T(512)S(1)}, s32[512]{0:T(512)}, u32[]{:S(2)}) copy-start(s32[512]{0:T(512)} %param.18) | copy-start | bytes 6148
  6.5 48.8 %all-gather.9.cloned.1.call-start = ((), (), s32[]{:S(2)}) async-start(), calls=%async_computation.2 | async-start | bytes 1802240 | tf_op jit(solution)/shard_map/all_gather | solution.py:102
  7.3 164.5 %all-gather.5.cloned.1.call-start = ((), (), s32[]{:S(2)}) async-start(), calls=%async_computation | async-start | bytes 7077888 | tf_op jit(solution)/shard_map/all_gather | solution.py:87
  33.6 176.3 %all-gather.7.cloned.1.call-start = ((), (), s32[]{:S(2)}) async-start(), calls=%async_computation.1 | async-start | bytes 2359296 | tf_op jit(solution)/shard_map/all_gather | solution.py:97
  52.6 237.8 %all-gather.11.cloned.1.call-start = ((), (), s32[]{:S(2)}) async-start(), calls=%async_computation.3 | async-start | bytes 6488064 | tf_op jit(solution)/shard_map/all_gather | solution.py:139
  55.4 45.8 %collective-permute-start.1 = (bf16[2,128,2816]{1,2,0:T(8,128)(2,1)}, bf16[2,128,2816]{1,2,0:T(8,128)(2,1)S(1)}, u32[]{:S(2)}, u32[]{:S(2)}) collective-permute-start(bf16[2,128,2816]{1,2,0:T(8,128)(2,1)} %all-gather.9.cloned.1.call-done), channel_id=1, source_target_pairs={{0,4},{4,8},{8,12},{12,16},{16,20},{20,24},{24,28},{28,0},{1,5},{5... | collective-permute-start | bytes 4325384 | tf_op jit(solution)/shard_map/ppermute | solution.py:116
  55.4 51.0 %collective-permute-start = (bf16[2,128,2816]{1,2,0:T(8,128)(2,1)}, bf16[2,128,2816]{1,2,0:T(8,128)(2,1)S(1)}, u32[]{:S(2)}, u32[]{:S(2)}) collective-permute-start(bf16[2,128,2816]{1,2,0:T(8,128)(2,1)} %all-gather.9.cloned.1.call-done), channel_id=1, source_target_pairs={{0,28},{4,0},{8,4},{12,8},{16,12},{20,16},{24,20},{28,24},{1,29},{... | collective-permute-start | bytes 4325384 | tf_op jit(solution)/shard_map/ppermute | solution.py:118
  102.3 45.7 %collective-permute-start.3 = (bf16[2,128,2816]{1,2,0:T(8,128)(2,1)S(1)}, bf16[2,128,2816]{1,2,0:T(8,128)(2,1)S(1)}, u32[]{:S(2)}, u32[]{:S(2)}) collective-permute-start(bf16[2,128,2816]{1,2,0:T(8,128)(2,1)S(1)} %collective-permute-done.1), channel_id=1, source_target_pairs={{0,4},{4,8},{8,12},{12,16},{16,20},{20,24},{24,28},{28,0},{1,5},{5... | collective-permute-start | bytes 4325384 | tf_op jit(solution)/shard_map/ppermute | solution.py:116
  106.4 71.7 %copy-start.3 = (bf16[2,128,2816]{1,2,0:T(8,128)(2,1)}, bf16[2,128,2816]{1,2,0:T(8,128)(2,1)S(1)}, u32[]{:S(2)}) copy-start(bf16[2,128,2816]{1,2,0:T(8,128)(2,1)S(1)} %collective-permute-done) | copy-start | bytes 4325380
  106.4 63.1 %collective-permute-start.2 = (bf16[2,128,2816]{1,2,0:T(8,128)(2,1)S(1)}, bf16[2,128,2816]{1,2,0:T(8,128)(2,1)}, u32[]{:S(2)}, u32[]{:S(2)}) collective-permute-start(bf16[2,128,2816]{1,2,0:T(8,128)(2,1)S(1)} %collective-permute-done), channel_id=1, source_target_pairs={{0,28},{4,0},{8,4},{12,8},{16,12},{20,16},{24,20},{28,24},{1,29},{... | collective-permute-start | bytes 4325384 | tf_op jit(solution)/shard_map/ppermute | solution.py:118
  148.1 23.7 %copy-start.5 = (bf16[2,128,2816]{1,2,0:T(8,128)(2,1)}, bf16[2,128,2816]{1,2,0:T(8,128)(2,1)S(1)}, u32[]{:S(2)}) copy-start(bf16[2,128,2816]{1,2,0:T(8,128)(2,1)S(1)} %collective-permute-done.3) | copy-start | bytes 4325380
  148.1 23.7 %collective-permute-start.5 = (bf16[2,128,2816]{1,2,0:T(8,128)(2,1)S(1)}, bf16[2,128,2816]{1,2,0:T(8,128)(2,1)}, u32[]{:S(2)}, u32[]{:S(2)}) collective-permute-start(bf16[2,128,2816]{1,2,0:T(8,128)(2,1)S(1)} %collective-permute-done.3), channel_id=1, source_target_pairs={{0,4},{4,8},{8,12},{12,16},{16,20},{20,24},{24,28},{28,0},{1,5},{5... | collective-permute-start | bytes 4325384 | tf_op jit(solution)/shard_map/ppermute | solution.py:116
  169.5 83.0 %collective-permute-start.4 = (bf16[2,128,2816]{1,2,0:T(8,128)(2,1)}, bf16[2,128,2816]{1,2,0:T(8,128)(2,1)}, u32[]{:S(2)}, u32[]{:S(2)}) collective-permute-start(bf16[2,128,2816]{1,2,0:T(8,128)(2,1)} %collective-permute-done.2), channel_id=1, source_target_pairs={{0,28},{4,0},{8,4},{12,8},{16,12},{20,16},{24,20},{28,24},{1,29},{... | collective-permute-start | bytes 4325384 | tf_op jit(solution)/shard_map/ppermute | solution.py:118
  171.7 87.9 %collective-permute-start.6 = (bf16[2,128,2816]{1,2,0:T(8,128)(2,1)}, bf16[2,128,2816]{1,2,0:T(8,128)(2,1)}, u32[]{:S(2)}, u32[]{:S(2)}) collective-permute-start(bf16[2,128,2816]{1,2,0:T(8,128)(2,1)} %collective-permute-done.5), channel_id=1, source_target_pairs={{0,4},{4,8},{8,12},{12,16},{16,20},{20,24},{24,28},{28,0},{1,5},{5... | collective-permute-start | bytes 4325384 | tf_op jit(solution)/shard_map/ppermute | solution.py:116
  189.8 9.0 %copy-start.8 = (bf16[1,512,1024]{1,2,0:T(8,128)(2,1)S(1)}, bf16[1,512,1024]{1,2,0:T(8,128)(2,1)}, u32[]{:S(2)}) copy-start(bf16[1,512,1024]{1,2,0:T(8,128)(2,1)} %copy.24) | copy-start | bytes 3145732
  198.8 11.1 %copy-start.7 = (bf16[512,1024]{1,0:T(8,128)(2,1)S(1)}, bf16[512,1024]{1,0:T(8,128)(2,1)}, u32[]{:S(2)}) copy-start(bf16[512,1024]{1,0:T(8,128)(2,1)} %param.10) | copy-start | bytes 3145732
  210.0 3.9 %copy-start.6 = (bf16[2,128,2816]{1,2,0:T(8,128)(2,1)S(1)}, bf16[2,128,2816]{1,2,0:T(8,128)(2,1)}, u32[]{:S(2)}) copy-start(bf16[2,128,2816]{1,2,0:T(8,128)(2,1)} %copy-done.5) | copy-start | bytes 4325380
  219.8 7.6 %copy-start.2 = (bf16[2,128,2816]{1,2,0:T(8,128)(2,1)S(1)}, bf16[2,128,2816]{1,2,0:T(8,128)(2,1)}, u32[]{:S(2)}) copy-start(bf16[2,128,2816]{1,2,0:T(8,128)(2,1)} %copy-done.1) | copy-start | bytes 4325380
  227.4 5.9 %copy-start.4 = (bf16[2,128,2816]{1,2,0:T(8,128)(2,1)S(1)}, bf16[2,128,2816]{1,2,0:T(8,128)(2,1)}, u32[]{:S(2)}) copy-start(bf16[2,128,2816]{1,2,0:T(8,128)(2,1)} %copy-done.3) | copy-start | bytes 4325380
  239.1 7.5 %copy-start = (bf16[2,128,2816]{1,2,0:T(8,128)(2,1)S(1)}, bf16[2,128,2816]{1,2,0:T(8,128)(2,1)}, u32[]{:S(2)}) copy-start(bf16[2,128,2816]{1,2,0:T(8,128)(2,1)} %all-gather.9.cloned.1.call-done) | copy-start | bytes 4325380
  (1 other events, 1.1 us)
Sparse Core Ops, SparseCore 0:
  8.9 46.3 all-gather.8
  57.3 66.0 all-gather.4
  125.3 33.5 all-gather.6
  166.5 60.6 all-gather.10
